TPU v7x, 32 devices: a whole 2x2x4 slice. The times are simulated.
32 devices in a mesh: shot: 2 (over x), mp: 16 (over z, y, core).
Axes of the slice: x: 2, y: 2, z: 4, core: 2. Of those that a mesh axis runs over, the one named last changes fastest.
Arguments:
- gradient_parts: float32 [8, 1024, 1024], P('shot', 'mp')
- history_s: bfloat16 [10, 1024, 1024], P(None, 'mp'), may hold values from -6 to 6
- history_y: bfloat16 [10, 1024, 1024], P(None, 'mp'), as said below
Outputs:
- direction: float32 [1024, 1024], P('mp', 'shot')
Inputs may be any that keep to these rules, and one draw needn't show every extreme that they name: In every cell, history_y[i] equals history_s[i] times a factor between 0.5 and 4.
All inputs are finite; a program needn't handle non-finite values.
Results may differ from a plain program's by a relative error of at most 0.0003.
Values sent between devices are 32-bit elements; how exact they have to be, the bound alone decides.
A program may use at most 64 MiB of HBM per device.

v0:
```python
import jax
import jax.numpy as jnp
from jax import lax
from jax.sharding import PartitionSpec as P

M = 10


def from_gram(gradient, steps, changes):
    shape = gradient.shape
    flat_grad = gradient.reshape(-1)
    stacked = jnp.concatenate([steps.reshape(M, -1), changes.reshape(M, -1)], axis=0)
    hist_gram = lax.dot_general(
        stacked, stacked, (((1,), (1,)), ((), ())), preferred_element_type=jnp.float32
    )
    stacked_wide = stacked.astype(jnp.float32)
    cross = jnp.dot(stacked_wide, flat_grad, precision=lax.Precision.HIGHEST)
    grad_sq = jnp.sum(flat_grad * flat_grad)
    top = jnp.concatenate([hist_gram, cross[:, None]], axis=1)
    bottom = jnp.concatenate([cross, grad_sq[None]])[None, :]
    gram = lax.psum(jnp.concatenate([top, bottom], axis=0), ("shot", "mp"))
    coeffs = jnp.zeros((2 * M + 1,), jnp.float32).at[2 * M].set(1.0)
    alphas = [None] * M
    for i in reversed(range(M)):
        rho_i = 1.0 / gram[i, M + i]
        alphas[i] = rho_i * jnp.dot(gram[i], coeffs, precision=lax.Precision.HIGHEST)
        coeffs = coeffs.at[M + i].add(-alphas[i])
    coeffs = coeffs * (gram[M - 1, 2 * M - 1] / gram[2 * M - 1, 2 * M - 1])
    for i in range(M):
        rho_i = 1.0 / gram[i, M + i]
        beta = rho_i * jnp.dot(gram[M + i], coeffs, precision=lax.Precision.HIGHEST)
        coeffs = coeffs.at[i].add(alphas[i] - beta)
    combined = (
        jnp.dot(coeffs[: 2 * M], stacked_wide, precision=lax.Precision.HIGHEST)
        + coeffs[2 * M] * flat_grad
    )
    return -combined.reshape(shape)


def shards(gradient_parts, history_s, history_y):
    partial_grad = jnp.sum(gradient_parts, axis=0)
    columns = partial_grad.shape[1] // lax.axis_size("shot")
    start = lax.axis_index("shot") * columns
    gradient = lax.psum_scatter(partial_grad, "shot", scatter_dimension=1, tiled=True)
    steps = lax.dynamic_slice_in_dim(history_s, start, columns, 2)
    changes = lax.dynamic_slice_in_dim(history_y, start, columns, 2)
    result = from_gram(gradient, steps, changes)
    return result


def solution(mesh):
    placed = (P("shot", "mp", None), P(None, "mp", None), P(None, "mp", None))
    return jax.shard_map(
        shards, mesh=mesh, in_specs=placed, out_specs=P("mp", "shot"), check_vma=False
    )
```

profile of v0, /device:TPU:0, one launch (start us, length us, event | category | flops | bytes accessed | tf_op | source)
XLA Modules:
  0.0 115.3 jit_solution(11096996644224984904)
XLA Ops:
  6.5 2.1 %reduce_sum.18 = f32[64,1024]{1,0:T(8,128)} reduce(f32[4,64,1024]{2,1,0:T(8,128)} %param.45, f32[]{:T(128)} %constant.493.clone.1), dimensions={0}, to_apply=%region_0.0 | reduce | flops 196608 | bytes 1310724 | tf_op jit(solution)/shard_map/reduce_sum | solution.py:41
  8.7 1.2 %constant_dynamic-slice_fusion = (bf16[10,64,512]{2,1,0:T(8,128)(2,1)S(1)}, bf16[10,64,512]{2,1,0:T(8,128)(2,1)S(1)}) fusion(bf16[10,64,1024]{2,1,0:T(8,128)(2,1)S(1)} %copy-done.1, s32[]{:T(128)S(6)} %select_n.4, bf16[10,64,1024]{2,1,0:T(8,128)(2,1)} %param.46), kind=kLoop, calls=%fused_computation.25 | loop fusion | bytes 2621444 | tf_op jit(solution)/shard_map/dynamic_slice | solution.py:46
  11.3 0.9 fusion.4
  12.2 11.9 %reduce-scatter.2.cloned.1.call-done = f32[64,512]{1,0:T(8,128)} async-done(((f32[64,1024]{1,0:T(8,128)}), f32[64,512]{1,0:T(8,128)}) %reduce-scatter.2.cloned.1.call-update) | async-done | bytes 131088 | tf_op jit(solution)/shard_map/reduce_scatter | solution.py:44
  24.1 1.1 copy.49
  25.2 1.7 %fusion.3 = f32[1,20]{1,0:T(1,128)S(1)} fusion(f32[32768,1]{0,1:T(1,128)S(1)} %bitcast.66, bf16[10,32768]{1,0:T(8,128)(2,1)S(1)} %bitcast.62, bf16[10,32768]{1,0:T(8,128)(2,1)S(1)} %bitcast.59), kind=kOutput, calls=%fused_computation.71 | convolution fusion | flops 10485760 | bytes 1441872 | tf_op jit(solution)/shard_map/dot_general | solution.py:17
  26.9 0.7 multiply_reduce_fusion
  27.6 0.7 maximum_bitcast_fusion
  28.5 39.4 %psum.7 = f32[21,21]{0,1:T(8,128)S(1)} all-reduce(f32[21,21]{0,1:T(8,128)S(1)} %pad_maximum_fusion.1), channel_id=1, replica_groups=mesh['shot'=2,'mp'=16] {'shot','mp'}, use_global_device_ids=true, to_apply=%region_3.0 | all-reduce | flops 441 | bytes 3528 | tf_op jit(solution)/shard_map/psum | solution.py:21
  67.9 0.7 fusion.5
  71.8 0.7 multiply_reduce_fusion.19
  77.8 0.7 multiply_reduce_fusion.16
  79.9 0.6 multiply_reduce_fusion.15
  82.1 0.7 multiply_reduce_fusion.14
  84.3 0.7 multiply_reduce_fusion.13
  86.5 0.6 multiply_reduce_fusion.12
  88.5 0.6 multiply_reduce_fusion.11
  91.3 0.6 multiply_reduce_fusion.10
  92.6 0.6 multiply_reduce_fusion.9
  94.0 0.6 multiply_reduce_fusion.8
  95.4 0.6 multiply_reduce_fusion.7
  105.2 1.2 %fusion = f32[1,32768]{1,0:T(1,128)S(1)} fusion(f32[21]{0:T(128)S(1)} %constant_dynamic-update-slice_fusion.1, bf16[10,32768]{1,0:T(8,128)(2,1)S(1)} %bitcast.63, bf16[10,32768]{1,0:T(8,128)(2,1)S(1)} %bitcast.60), kind=kOutput, calls=%fused_computation.28 | convolution fusion | flops 10485760 | bytes 1441876 | tf_op jit(solution)/shard_map/dot_general | solution.py:34
  107.1 0.7 add_negate_fusion
  107.7 0.7 neg.47
  (48 shorter events, 11.1 us)
Async XLA Ops:
  6.5 2.1 %copy-start.1 = (bf16[10,64,1024]{2,1,0:T(8,128)(2,1)S(1)}, bf16[10,64,1024]{2,1,0:T(8,128)(2,1)}, u32[]{:S(2)}) copy-start(bf16[10,64,1024]{2,1,0:T(8,128)(2,1)} %param.47) | copy-start | bytes 3932164
  6.5 17.5 %reduce-scatter.2.cloned.1.call-start = ((), (), s32[]{:S(2)}) async-start(), calls=%async_computation.1 | async-start | bytes 393216 | tf_op jit(solution)/shard_map/reduce_scatter | solution.py:44
  10.7 0.7 copy-start.2
  24.1 2.9 %copy-start = (f32[64,512]{1,0:T(8,128)S(1)}, f32[64,512]{1,0:T(8,128)}, u32[]{:S(2)}) copy-start(f32[64,512]{1,0:T(8,128)} %reduce-scatter.2.cloned.1.call-done) | copy-start | bytes 393220
Sparse Core Ops, SparseCore 0:
  9.6 14.4 reduce-scatter.1
where the time goes:
time: 116 us; the launch traced here: 115 us
  blocking collectives  39.4 us (34%)
  between operations  34.3 us (30%)
  other arithmetic  19.3 us (17%)
  waiting for transfers between devices  11.9 us (10%)
  local copies, waits for them, and re-layouts  6.54 us (6%)
  matrix products  3.83 us (3%)
    psum x1, blocking collectives, from_gram(): gram = lax.psum(jnp.concatenate([top, bottom], axis=0), ('shot', 'mp'))  39.4 us
    reduce_scatter x1, waiting for transfers between devices, shards(): lax.psum_scatter(partial_grad, 'shot', scatter_dimension=1, tiled=True)  11.9 us
    dot_general x10, other arithmetic, from_gram(): jnp.dot(gram[i], coeffs, precision=lax.Precision.HIGHEST)  6.32 us
    dot_general x10, other arithmetic, from_gram(): beta = rho_i * jnp.dot(gram[M + i], coeffs, precision=lax.Precision.HIGHEST)  6.05 us
    unnamed x13, local copies, waits for them, and re-layouts  2.55 us
  transfers between devices with their start and end apart: 1, of which 1 were waited for; matrix products, arithmetic and copies ran while one was open for 3% of the time, Pallas kernels for 0%

commit v1 on v0

v1 whole, which is shorter than its diff:
```python
import functools

import jax
import jax.numpy as jnp
from jax import lax
from jax.experimental import pallas as pl
from jax.experimental.pallas import tpu as pltpu
from jax.sharding import PartitionSpec as P

M = 10
G = 16
MESH = pl.DeviceIdType.MESH


def place(a, b):
    return a % 8, G * (b % 8) + (a // 8) * 2 + b // 8


def pack(acc, n_shot):
    lanes = acc.shape[1]
    row = lax.broadcasted_iota(jnp.int32, acc.shape, 0) % G
    col = lax.broadcasted_iota(jnp.int32, acc.shape, 1) % G
    kept = jnp.where(row == col, acc, 0.0)
    sums = jnp.sum(kept.reshape(2 * M, G, lanes), axis=1)
    sums = jnp.concatenate([sums, jnp.zeros((24 - 2 * M, lanes), jnp.float32)], axis=0)
    for shift in (8, 4, 2, 1):
        sums = sums + pltpu.roll(sums, lanes - shift, 1)
    wide = sums + pltpu.roll(sums, lanes - G, 1) + pltpu.roll(sums, lanes - 2 * G, 1)
    group = lax.broadcasted_iota(jnp.int32, sums.shape, 1) // G
    sums = jnp.where(group == M, wide, sums * (1.0 / n_shot))
    lane = lax.broadcasted_iota(jnp.int32, (8, 128), 1) % G
    packed = jnp.zeros((8, 128), jnp.float32)
    for p in range(3):
        for q in range(2):
            piece = sums[8 * p : 8 * p + 8, 128 * q : 128 * q + 128]
            index = 2 * p + q
            if index:
                piece = pltpu.roll(piece, index, 1)
            packed = jnp.where(lane == index, piece, packed)
    return packed


def two_loop(get, inv):
    alphas = [None] * M
    left = [get(i, M) for i in range(M)]
    for j in reversed(range(M)):
        alphas[j] = left[j] * inv(j, j)
        for i in range(j):
            left[i] = left[i] - alphas[j] * get(i, j)
    gamma = get(M - 1, M - 1) * inv(2 * M - 1, M - 1)
    moved = []
    for i in range(M):
        dot = get(M + i, M)
        for j in range(M):
            dot = dot - alphas[j] * get(M + i, j)
        moved.append(gamma * dot)
    deltas = [None] * M
    for i in range(M):
        deltas[i] = alphas[i] - moved[i] * inv(i, i)
        for k in range(i + 1, M):
            moved[k] = moved[k] + deltas[i] * get(i, k)
    return deltas, [-gamma * a for a in alphas], gamma


def kernel(
    n_shot, n_mp, parts_hbm, s_hbm, y_hbm, out_ref,
    parts, s_all, y_all, partial, others, acc, mine, blocks, half, halves, scalars, tot,
    in_sem, g_send, g_recv, a_send, a_recv, b_send, b_recv, s_sem,
):
    shot, mp = lax.axis_index("shot"), lax.axis_index("mp")
    rows, width = parts.shape[1], parts.shape[2]
    cols = width // n_shot
    groups = rows // G

    def load(hbm, vmem, which, r):
        span = pl.ds(r * G, G)
        return pltpu.make_async_copy(hbm.at[:, span, :], vmem.at[:, span, :], in_sem.at[which, r])

    loads = []
    for r in range(groups):
        loads.append((load(parts_hbm, parts, 0, r), load(s_hbm, s_all, 1, r), load(y_hbm, y_all, 2, r)))
        for copy in loads[-1]:
            copy.start()

    barrier = pltpu.get_barrier_semaphore()
    for k in range(1, n_mp):
        pl.semaphore_signal(barrier, inc=1, device_id={"mp": lax.rem(mp + k, n_mp)}, device_id_type=MESH)
    for k in range(1, n_shot):
        pl.semaphore_signal(barrier, inc=1, device_id={"shot": lax.rem(shot + k, n_shot)}, device_id_type=MESH)

    for r in range(groups):
        for copy in loads[r]:
            copy.wait()
        span = slice(r * G, r * G + G)
        grad = parts[0, span, :]
        for i in range(1, parts.shape[0]):
            grad = grad + parts[i, span, :]
        for p in range(n_shot):
            partial[p, span, :] = grad[:, p * cols : p * cols + cols]
        high = grad.astype(jnp.bfloat16)
        rest = grad - high.astype(jnp.float32)
        mid = rest.astype(jnp.bfloat16)
        low = (rest - mid.astype(jnp.float32)).astype(jnp.bfloat16)
        s = s_all[:, span, :].reshape(M * G, width)
        y = y_all[:, span, :].reshape(M * G, width)
        left = jnp.concatenate([s, y], axis=0)
        right = jnp.concatenate([y, high, mid, low, jnp.zeros((3 * G, width), jnp.bfloat16)], axis=0)
        prod = lax.dot_general(left, right, (((1,), (1,)), ((), ())), preferred_element_type=jnp.float32)
        if r == 0:
            acc[...] = prod
        else:
            acc[...] += prod

    pl.semaphore_wait(barrier, n_mp + n_shot - 2)
    g_copies = []
    for k in range(1, n_shot):
        to = lax.rem(shot + k, n_shot)
        copy = pltpu.make_async_remote_copy(
            src_ref=partial.at[to], dst_ref=others.at[shot], send_sem=g_send.at[k], recv_sem=g_recv.at[shot],
            device_id={"shot": to}, device_id_type=MESH,
        )
        copy.start()
        g_copies.append(copy)

    packed = pack(acc[...], n_shot)
    mine[...] = packed

    def spread(src, dst, axis, me, n, send, recv):
        copies = []
        for k in range(1, n):
            copy = pltpu.make_async_remote_copy(
                src_ref=src, dst_ref=dst.at[me], send_sem=send.at[k], recv_sem=recv.at[me],
                device_id={axis: lax.rem(me + k, n)}, device_id_type=MESH,
            )
            copy.start()
            copies.append(copy)
        return copies

    def arrive(src, dst, axis, me, n, send, recv):
        for k in range(1, n):
            frm = lax.rem(me + k, n)
            pltpu.make_async_remote_copy(
                src_ref=src, dst_ref=dst.at[frm], send_sem=send.at[k], recv_sem=recv.at[frm],
                device_id={axis: frm}, device_id_type=MESH,
            ).wait_recv()

    a_copies = spread(mine, blocks, "mp", mp, n_mp, a_send, a_recv)
    blocks[mp] = packed
    arrive(mine, blocks, "mp", mp, n_mp, a_send, a_recv)
    total = blocks[0]
    for p in range(1, n_mp):
        total = total + blocks[p]
    half[...] = total
    b_copies = spread(half, halves, "shot", shot, n_shot, b_send, b_recv)
    halves[shot] = total
    arrive(half, halves, "shot", shot, n_shot, b_send, b_recv)
    total = halves[0]
    for p in range(1, n_shot):
        total = total + halves[p]
    tot[0] = total
    tot[1] = 1.0 / total
    copy = pltpu.make_async_copy(tot, scalars, s_sem)
    copy.start()
    copy.wait()

    def get(a, b):
        i, j = place(a, b)
        return scalars[0, i, j]

    def inv(a, b):
        i, j = place(a, b)
        return scalars[1, i, j]

    c_s, c_y, c_g = two_loop(get, inv)
    for k in range(1, n_shot):
        frm = lax.rem(shot + k, n_shot)
        pltpu.make_async_remote_copy(
            src_ref=partial.at[frm], dst_ref=others.at[frm], send_sem=g_send.at[k], recv_sem=g_recv.at[frm],
            device_id={"shot": frm}, device_id_type=MESH,
        ).wait_recv()
    own = pl.ds(pl.multiple_of(shot * cols, cols), cols)
    for r in range(groups):
        span = slice(r * G, r * G + G)
        grad = partial[shot, span, :]
        for k in range(1, n_shot):
            grad = grad + others[lax.rem(shot + k, n_shot), span, :]
        result = -c_g * grad
        for i in range(M):
            result = result - c_y[i] * y_all[i, span, own].astype(jnp.float32)
            result = result - c_s[i] * s_all[i, span, own].astype(jnp.float32)
        out_ref[span, :] = result
    for copy in g_copies + a_copies + b_copies:
        copy.wait_send()


def solution(mesh):
    n_shot, n_mp = mesh.shape["shot"], mesh.shape["mp"]

    def step(parts, s, y):
        shots, rows, width = parts.shape
        cols = width // n_shot
        dma = pltpu.SemaphoreType.DMA
        return pl.pallas_call(
            functools.partial(kernel, n_shot, n_mp),
            out_shape=jax.ShapeDtypeStruct((rows, cols), jnp.float32),
            in_specs=[pl.BlockSpec(memory_space=pl.ANY)] * 3,
            out_specs=pl.BlockSpec(memory_space=pltpu.VMEM),
            scratch_shapes=[
                pltpu.VMEM((shots, rows, width), jnp.float32),
                pltpu.VMEM((M, rows, width), jnp.bfloat16),
                pltpu.VMEM((M, rows, width), jnp.bfloat16),
                pltpu.VMEM((n_shot, rows, cols), jnp.float32),
                pltpu.VMEM((n_shot, rows, cols), jnp.float32),
                pltpu.VMEM((2 * M * G, 256), jnp.float32),
                pltpu.VMEM((8, 128), jnp.float32),
                pltpu.VMEM((n_mp, 8, 128), jnp.float32),
                pltpu.VMEM((8, 128), jnp.float32),
                pltpu.VMEM((n_shot, 8, 128), jnp.float32),
                pltpu.SMEM((2, 8, 128), jnp.float32),
                pltpu.VMEM((2, 8, 128), jnp.float32),
                dma((3, rows // G)),
                dma((n_shot,)),
                dma((n_shot,)),
                dma((n_mp,)),
                dma((n_mp,)),
                dma((n_shot,)),
                dma((n_shot,)),
                dma,
            ],
            compiler_params=pltpu.CompilerParams(collective_id=0, has_side_effects=True),
        )(parts, s, y)

    placed = (P("shot", "mp", None), P(None, "mp", None), P(None, "mp", None))
    return jax.shard_map(step, mesh=mesh, in_specs=placed, out_specs=P("mp", "shot"), check_vma=False)
```

time: 116 us -> 18.2 us (0.16)
  blocking collectives: 39.4 us -> 0 us
  between operations: 34.3 us -> 0.01 us
  other arithmetic: 19.3 us -> 0 us
  Pallas kernels: 0 us -> 16.5 us
  waiting for transfers between devices: 11.9 us -> 0 us
  local copies, waits for them, and re-layouts: 6.54 us -> 1.57 us
  matrix products: 3.83 us -> 0 us
    psum x1 -> x0, blocking collectives: 39.4 us -> none  [from_gram(): gram = lax.psum(jnp.concatenate([top, bottom], axis=0), ('shot', 'mp'))]
    pallas_call x0 -> x1, Pallas kernels: none -> 16.5 us  [step(): pl.pallas_call(functools.partial(kernel, n_shot, n_mp), out_shape=jax.Sha...]
    dot_general x20 -> x0, other arithmetic: 12.4 us -> none  [the longest x10 6.32 us: from_gram(): jnp.dot(gram[i], coeffs, precision=lax.Precision.HIGHEST)]
    reduce_scatter x1 -> x0, waiting for transfers between devices: 11.9 us -> none  [shards(): lax.psum_scatter(partial_grad, 'shot', scatter_dimension=1, tiled=True)]
    dot_general x3 -> x0, matrix products: 3.83 us -> none  [the longest x1 1.73 us: from_gram(): cross = jnp.dot(stacked_wide, flat_grad, precision=lax.Precision.HIGHEST)]
    reduce_sum x2 -> x0, other arithmetic: 2.75 us -> none  [the longest x1 2.1 us: shards(): partial_grad = jnp.sum(gradient_parts, axis=0)]
    scatter-add x19 -> x0, other arithmetic: 2.73 us -> none  [the longest x10 1.38 us: from_gram(): coeffs = coeffs.at[i].add(alphas[i] - beta)]
    slice x4 -> x0, local copies, waits for them, and re-layouts: 2 us -> none  [the longest x1 0.7 us: from_gram(): coeffs = coeffs * (gram[M - 1, 2 * M - 1] / gram[2 * M - 1, 2 * M - 1])]
  transfers between devices with their start and end apart: 1 -> 0, of which waited for: 1 -> 0; matrix products, arithmetic and copies ran while one was open for 3% -> 0% of each run, Pallas kernels for 0% -> 0%
where the time goes in v1:
time: 18.2 us; the launch traced here: 18.1 us
  Pallas kernels  16.5 us (91%)
  local copies, waits for them, and re-layouts  1.57 us (9%)
    pallas_call x1, Pallas kernels, step(): pl.pallas_call(functools.partial(kernel, n_shot, n_mp), out_shape=jax.Sha...  16.5 us
    unnamed x1, local copies, waits for them, and re-layouts  1.57 us

profile of v1, /device:TPU:0, one launch (start us, length us, event | category | flops | bytes accessed | tf_op | source)
XLA Modules:
  0.0 18.1 jit_solution(9603986047125494535)
XLA Ops:
  0.0 16.5 %shard_map.37 = f32[64,512]{1,0:T(8,128)} custom-call(f32[4,64,1024]{2,1,0:T(8,128)} %parts_hbm.1, bf16[10,64,1024]{2,1,0:T(8,128)(2,1)} %s_hbm.1, bf16[10,64,1024]{2,1,0:T(8,128)(2,1)} %y_hbm.1), custom_call_target="tpu_custom_call" | custom-call | tf_op jit(solution)/shard_map/pallas_call | solution.py:203
  16.5 1.6 %copy.5 = f32[64,512]{1,0:T(8,128)} copy(f32[64,512]{1,0:T(8,128)} %shard_map.37) | data formatting | bytes 262144

commit v2 on v1

--- a/solution.py
+++ b/solution.py
@@ -64,8 +64,8 @@
 
 def kernel(
     n_shot, n_mp, parts_hbm, s_hbm, y_hbm, out_ref,
-    parts, s_all, y_all, partial, others, acc, mine, blocks, half, halves, scalars, tot,
-    in_sem, g_send, g_recv, a_send, a_recv, b_send, b_recv, s_sem,
+    parts, s_all, y_all, partial, others, acc, mine, blocks, scalars, tot,
+    in_sem, g_send, g_recv, a_send, a_recv, s_sem,
 ):
     shot, mp = lax.axis_index("shot"), lax.axis_index("mp")
     rows, width = parts.shape[1], parts.shape[2]
@@ -76,27 +76,36 @@
         span = pl.ds(r * G, G)
         return pltpu.make_async_copy(hbm.at[:, span, :], vmem.at[:, span, :], in_sem.at[which, r])
 
-    loads = []
-    for r in range(groups):
-        loads.append((load(parts_hbm, parts, 0, r), load(s_hbm, s_all, 1, r), load(y_hbm, y_all, 2, r)))
-        for copy in loads[-1]:
-            copy.start()
+    sources = ((parts_hbm, parts), (s_hbm, s_all), (y_hbm, y_all))
+    loads = [[load(*sources[w], w, r) for w in range(3)] for r in range(groups)]
+    for r in range(groups):
+        loads[r][0].start()
+    for r in range(groups):
+        loads[r][1].start()
+        loads[r][2].start()
 
     barrier = pltpu.get_barrier_semaphore()
-    for k in range(1, n_mp):
-        pl.semaphore_signal(barrier, inc=1, device_id={"mp": lax.rem(mp + k, n_mp)}, device_id_type=MESH)
-    for k in range(1, n_shot):
-        pl.semaphore_signal(barrier, inc=1, device_id={"shot": lax.rem(shot + k, n_shot)}, device_id_type=MESH)
-
-    for r in range(groups):
-        for copy in loads[r]:
-            copy.wait()
-        span = slice(r * G, r * G + G)
-        grad = parts[0, span, :]
-        for i in range(1, parts.shape[0]):
-            grad = grad + parts[i, span, :]
+    for d in range(n_shot):
+        for k in range(n_mp):
+            if d or k:
+                to = {"shot": lax.rem(shot + d, n_shot), "mp": lax.rem(mp + k, n_mp)}
+                pl.semaphore_signal(barrier, inc=1, device_id=to, device_id_type=MESH)
+
+    for r in range(groups):
+        loads[r][0].wait()
+        span = slice(r * G, r * G + G)
         for p in range(n_shot):
-            partial[p, span, :] = grad[:, p * cols : p * cols + cols]
+            part = slice(p * cols, p * cols + cols)
+            grad = parts[0, span, part]
+            for i in range(1, parts.shape[0]):
+                grad = grad + parts[i, span, part]
+            partial[p, span, :] = grad
+
+    for r in range(0, groups - 2):
+        loads[r][1].wait()
+        loads[r][2].wait()
+        span = slice(r * G, r * G + G)
+        grad = jnp.concatenate([partial[p, span, :] for p in range(n_shot)], axis=1)
         high = grad.astype(jnp.bfloat16)
         rest = grad - high.astype(jnp.float32)
         mid = rest.astype(jnp.bfloat16)
@@ -111,7 +120,7 @@
         else:
             acc[...] += prod
 
-    pl.semaphore_wait(barrier, n_mp + n_shot - 2)
+    pl.semaphore_wait(barrier, n_mp * n_shot - 1)
     g_copies = []
     for k in range(1, n_shot):
         to = lax.rem(shot + k, n_shot)
@@ -122,41 +131,52 @@
         copy.start()
         g_copies.append(copy)
 
+    for r in range(groups - 2, groups):
+        loads[r][1].wait()
+        loads[r][2].wait()
+        span = slice(r * G, r * G + G)
+        grad = jnp.concatenate([partial[p, span, :] for p in range(n_shot)], axis=1)
+        high = grad.astype(jnp.bfloat16)
+        rest = grad - high.astype(jnp.float32)
+        mid = rest.astype(jnp.bfloat16)
+        low = (rest - mid.astype(jnp.float32)).astype(jnp.bfloat16)
+        s = s_all[:, span, :].reshape(M * G, width)
+        y = y_all[:, span, :].reshape(M * G, width)
+        left = jnp.concatenate([s, y], axis=0)
+        right = jnp.concatenate([y, high, mid, low, jnp.zeros((3 * G, width), jnp.bfloat16)], axis=0)
+        prod = lax.dot_general(left, right, (((1,), (1,)), ((), ())), preferred_element_type=jnp.float32)
+        if r == 0:
+            acc[...] = prod
+        else:
+            acc[...] += prod
+
     packed = pack(acc[...], n_shot)
     mine[...] = packed
 
-    def spread(src, dst, axis, me, n, send, recv):
-        copies = []
-        for k in range(1, n):
-            copy = pltpu.make_async_remote_copy(
-                src_ref=src, dst_ref=dst.at[me], send_sem=send.at[k], recv_sem=recv.at[me],
-                device_id={axis: lax.rem(me + k, n)}, device_id_type=MESH,
-            )
-            copy.start()
-            copies.append(copy)
-        return copies
-
-    def arrive(src, dst, axis, me, n, send, recv):
-        for k in range(1, n):
-            frm = lax.rem(me + k, n)
-            pltpu.make_async_remote_copy(
-                src_ref=src, dst_ref=dst.at[frm], send_sem=send.at[k], recv_sem=recv.at[frm],
-                device_id={axis: frm}, device_id_type=MESH,
-            ).wait_recv()
-
-    a_copies = spread(mine, blocks, "mp", mp, n_mp, a_send, a_recv)
-    blocks[mp] = packed
-    arrive(mine, blocks, "mp", mp, n_mp, a_send, a_recv)
+    here = shot * n_mp + mp
+    a_copies = []
+    for d in range(n_shot):
+        for k in range(n_mp):
+            if d or k:
+                copy = pltpu.make_async_remote_copy(
+                    src_ref=mine, dst_ref=blocks.at[here], send_sem=a_send.at[d, k], recv_sem=a_recv.at[here],
+                    device_id={"shot": lax.rem(shot + d, n_shot), "mp": lax.rem(mp + k, n_mp)}, device_id_type=MESH,
+                )
+                copy.start()
+                a_copies.append(copy)
+    blocks[here] = packed
+    for d in range(n_shot):
+        for k in range(n_mp):
+            if d or k:
+                row, col = lax.rem(shot + d, n_shot), lax.rem(mp + k, n_mp)
+                frm = row * n_mp + col
+                pltpu.make_async_remote_copy(
+                    src_ref=mine, dst_ref=blocks.at[frm], send_sem=a_send.at[d, k], recv_sem=a_recv.at[frm],
+                    device_id={"shot": row, "mp": col}, device_id_type=MESH,
+                ).wait_recv()
     total = blocks[0]
-    for p in range(1, n_mp):
+    for p in range(1, n_shot * n_mp):
         total = total + blocks[p]
-    half[...] = total
-    b_copies = spread(half, halves, "shot", shot, n_shot, b_send, b_recv)
-    halves[shot] = total
-    arrive(half, halves, "shot", shot, n_shot, b_send, b_recv)
-    total = halves[0]
-    for p in range(1, n_shot):
-        total = total + halves[p]
     tot[0] = total
     tot[1] = 1.0 / total
     copy = pltpu.make_async_copy(tot, scalars, s_sem)
@@ -189,7 +209,7 @@
             result = result - c_y[i] * y_all[i, span, own].astype(jnp.float32)
             result = result - c_s[i] * s_all[i, span, own].astype(jnp.float32)
         out_ref[span, :] = result
-    for copy in g_copies + a_copies + b_copies:
+    for copy in g_copies + a_copies:
         copy.wait_send()
 
 
@@ -213,21 +233,17 @@
                 pltpu.VMEM((n_shot, rows, cols), jnp.float32),
                 pltpu.VMEM((2 * M * G, 256), jnp.float32),
                 pltpu.VMEM((8, 128), jnp.float32),
-                pltpu.VMEM((n_mp, 8, 128), jnp.float32),
-                pltpu.VMEM((8, 128), jnp.float32),
-                pltpu.VMEM((n_shot, 8, 128), jnp.float32),
+                pltpu.VMEM((n_shot * n_mp, 8, 128), jnp.float32),
                 pltpu.SMEM((2, 8, 128), jnp.float32),
                 pltpu.VMEM((2, 8, 128), jnp.float32),
                 dma((3, rows // G)),
                 dma((n_shot,)),
                 dma((n_shot,)),
-                dma((n_mp,)),
-                dma((n_mp,)),
-                dma((n_shot,)),
-                dma((n_shot,)),
+                dma((n_shot, n_mp)),
+                dma((n_shot * n_mp,)),
                 dma,
             ],
-            compiler_params=pltpu.CompilerParams(collective_id=0, has_side_effects=True),
+            compiler_params=pltpu.CompilerParams(collective_id=0, has_side_effects=True, vmem_limit_bytes=56_000_000),
         )(parts, s, y)
 
     placed = (P("shot", "mp", None), P(None, "mp", None), P(None, "mp", None))

time: 18.2 us -> 15.7 us (0.86)
  Pallas kernels: 16.5 us -> 14.9 us
  local copies, waits for them, and re-layouts: 1.57 us -> 0.66 us
    pallas_call x1, Pallas kernels: 16.5 us -> 14.9 us  [step(): pl.pallas_call(functools.partial(kernel, n_shot, n_mp), out_shape=jax.Sha...]
    unnamed x1, local copies, waits for them, and re-layouts: 1.57 us -> 0.66 us
where the time goes in v2:
time: 15.7 us; the launch traced here: 15.5 us
  Pallas kernels  14.9 us (95%)
  local copies, waits for them, and re-layouts  0.66 us (4%)
    pallas_call x1, Pallas kernels, step(): pl.pallas_call(functools.partial(kernel, n_shot, n_mp), out_shape=jax.Sha...  14.9 us
    unnamed x1, local copies, waits for them, and re-layouts  0.66 us

profile of v2, /device:TPU:0, one launch (start us, length us, event | category | flops | bytes accessed | tf_op | source)
XLA Modules:
  0.0 15.5 jit_solution(5270114785593828655)
XLA Ops:
  0.0 14.9 %shard_map.37 = f32[64,512]{1,0:T(8,128)S(1)} custom-call(f32[4,64,1024]{2,1,0:T(8,128)} %parts_hbm.1, bf16[10,64,1024]{2,1,0:T(8,128)(2,1)} %s_hbm.1, bf16[10,64,1024]{2,1,0:T(8,128)(2,1)} %y_hbm.1), custom_call_target="tpu_custom_call" | custom-call | tf_op jit(solution)/shard_map/pallas_call | solution.py:223
  14.9 0.7 %copy.5 = f32[64,512]{1,0:T(8,128)} copy(f32[64,512]{1,0:T(8,128)S(1)} %shard_map.37) | data formatting | bytes 262144
